TPU v7x, 32 devices: a whole 2x2x4 slice. The times are simulated.
32 devices in a mesh: grp: 4 (over x, core), lat: 8 (over z, y).
Axes of the slice: x: 2, y: 2, z: 4, core: 2. Of those that a mesh axis runs over, the one named last changes fastest.
Arguments:
- grid_state: bfloat16 [16, 192, 384, 128], P('grp', 'lat'), may hold values from -6 to 6
- noise_field: bfloat16 [16, 192, 384, 128], P('grp', 'lat'), may hold values from -6 to 6
- legendre: bfloat16 [192, 128, 128], P('lat'), may hold values from -0.4375 to 0.4375
- diffusion: float32 [128], replicated, may hold values from 0.1 to 10
- input_weight: bfloat16 [128, 256], replicated, may hold values from -0.5 to 0.5
- noise_weight: bfloat16 [128, 256], replicated, may hold values from -0.5 to 0.5
- input_bias: float32 [256], replicated, may hold values from -4 to 4
- middle_weight: bfloat16 [256, 256], replicated, may hold values from -0.375 to 0.375
- output_weight: bfloat16 [256, 128], replicated, may hold values from -0.375 to 0.375
Outputs:
- new_state: bfloat16 [16, 192, 384, 128], P('grp', 'lat')
- ens_mean: float32 [192, 384, 128], P('lat')
- ens_var: float32 [192, 384, 128], P('lat')
All inputs are finite; a program needn't handle non-finite values.
Results may differ from a plain program's by a relative error of at most 0.012.
Values may be sent and summed in bfloat16 or wider, within the bound.
A program may use at most 192 MiB of HBM per device.

v0:
```python
import math
import jax
import jax.numpy as jnp
from jax import lax
from jax.sharding import PartitionSpec as P


def wave_table(lon_count, wave_count):
    lon_ids = jnp.arange(lon_count, dtype=jnp.int32)[:, None]
    wave_ids = jnp.arange(wave_count, dtype=jnp.int32)[None, :]
    phase = (lon_ids * wave_ids % lon_count).astype(jnp.float32) * (2.0 * math.pi / lon_count)
    factor = math.sqrt(2.0 / lon_count)
    joined = jnp.concatenate([jnp.cos(phase), -jnp.sin(phase)], axis=1) * factor
    return joined.astype(jnp.bfloat16)


def damping_filter(diffusion, wave_count):
    degree = jnp.arange(wave_count, dtype=jnp.int32).astype(jnp.float32)
    ratio = degree * (degree + 1.0) / float((wave_count - 1) * wave_count)
    return 1.0 / (1.0 + diffusion[None, :] * (ratio * ratio)[:, None])


def per_device(
    grid_state,
    noise_field,
    legendre,
    diffusion,
    input_weight,
    noise_weight,
    input_bias,
    middle_weight,
    output_weight,
):
    members, lat_rows, lon_count, channels = grid_state.shape
    wave_count = legendre.shape[1]
    local_waves = wave_count // lax.axis_size("lat")
    transform = wave_table(lon_count, wave_count)
    fourier = jnp.einsum(
        "blxc,xk->blkc", grid_state, transform, preferred_element_type=jnp.float32
    ).astype(jnp.bfloat16)
    fourier = fourier.reshape(members, lat_rows, 2, wave_count, channels)
    basis_band = lax.all_to_all(legendre, "lat", split_axis=1, concat_axis=0, tiled=True)
    zonal_ids = lax.axis_index("lat") * local_waves + jnp.arange(local_waves, dtype=jnp.int32)
    total_ids = jnp.arange(wave_count, dtype=jnp.int32)
    triangle = (total_ids[None, :] >= zonal_ids[:, None]).astype(jnp.float32)
    damping = damping_filter(diffusion, wave_count)
    spectrum = jnp.einsum(
        "lmn,blrmc->brmnc",
        basis_band,
        lax.all_to_all(fourier, "lat", split_axis=3, concat_axis=1, tiled=True),
        preferred_element_type=jnp.float32,
    )
    spectrum = spectrum * triangle[None, None, :, :, None]
    filtered = (spectrum * damping[None, None, None, :, :]).astype(jnp.bfloat16)
    banded_grid = jnp.einsum(
        "lmn,brmnc->blrmc", basis_band, filtered, preferred_element_type=jnp.float32
    ).astype(jnp.bfloat16)
    grid_fourier = lax.all_to_all(banded_grid, "lat", split_axis=1, concat_axis=3, tiled=True)
    grid_fourier = grid_fourier.reshape(members, lat_rows, 2 * wave_count, channels)
    smoothed = jnp.einsum(
        "bljc,xj->blxc", grid_fourier, transform, preferred_element_type=jnp.float32
    )
    flat_fields = smoothed.reshape(-1, channels)
    smoothed_in = flat_fields.astype(jnp.bfloat16)
    pre_act = jnp.dot(smoothed_in, input_weight, preferred_element_type=jnp.float32)
    pre_act = pre_act + jnp.dot(
        noise_field.reshape(-1, noise_field.shape[3]),
        noise_weight,
        preferred_element_type=jnp.float32,
    )
    hidden_one = jax.nn.silu(pre_act + input_bias).astype(jnp.bfloat16)
    hidden_two = jax.nn.silu(
        jnp.dot(hidden_one, middle_weight, preferred_element_type=jnp.float32)
    ).astype(jnp.bfloat16)
    tendency = jnp.dot(hidden_two, output_weight, preferred_element_type=jnp.float32)
    new_state = (flat_fields + tendency).astype(jnp.bfloat16).reshape(grid_state.shape)
    member_values = new_state.astype(jnp.float32)
    ensemble = members * lax.axis_size("grp")
    summed = lax.psum(jnp.sum(member_values, axis=0).astype(jnp.bfloat16), "grp").astype(
        jnp.float32
    )
    ens_mean = summed / ensemble
    spread = lax.psum(
        jnp.sum(jnp.square(member_values - ens_mean), axis=0).astype(jnp.bfloat16), "grp"
    ).astype(jnp.float32)
    ens_var = spread / (ensemble - 1)
    return (new_state, ens_mean, ens_var)


def solution(mesh):
    in_specs = (
        P("grp", "lat", None, None),
        P("grp", "lat", None, None),
        P("lat", None, None),
        P(),
        P(),
        P(),
        P(),
        P(),
        P(),
    )
    out_specs = (P("grp", "lat", None, None), P("lat", None, None), P("lat", None, None))
    return jax.shard_map(
        per_device, mesh=mesh, in_specs=in_specs, out_specs=out_specs, check_vma=False
    )
```

profile of v0, /device:TPU:0, one launch (start us, length us, event | category | flops | bytes accessed | tf_op | source)
XLA Modules:
  0.0 592.4 jit_solution(8928592732857764437)
XLA Ops:
  7.2 2.6 copy.27
  9.7 7.3 %all-to-all-start.1 = ((bf16[24,128,128]{2,0,1:T(8,128)(2,1)}), bf16[24,128,128]{2,0,1:T(8,128)(2,1)S(1)}, u32[]{:S(2)}, u32[]{:S(2)}) async-start(bf16[24,128,128]{2,0,1:T(8,128)(2,1)} %copy.27), calls=%async_computation.1 | async-start | bytes 1572864 | tf_op jit(solution)/shard_map/all_to_all | solution.py:42
  17.9 7.4 %convolution_convert_fusion = bf16[256,4,24,128]{3,0,2,1:T(8,128)(2,1)S(1)} fusion(bf16[4,24,384,128]{3,2,1,0:T(8,128)(2,1)} %param.9, f32[384,128]{0,1:T(8,128)S(1)} %get-tuple-element.3, f32[384,128]{0,1:T(8,128)S(1)} %get-tuple-element.4), kind=kOutput, calls=%fused_computation.19 | convolution fusion | flops 2419359744 | bytes 16121856 | tf_op jit(solution)/shard_map/blxc,xk->blkc/dot_general | solution.py:38
  25.2 20.3 %copy.24 = bf16[4,24,2,128,128]{4,2,1,0,3:T(2,128)(2,1)} copy(bf16[4,24,2,128,128]{4,3,2,1,0:T(8,128)(2,1)S(1)} %bitcast.52) | data formatting | bytes 12582912 | tf_op jit(solution)/shard_map/reshape | solution.py:41
  45.6 6.1 %all-to-all-start = ((bf16[4,24,2,128,128]{4,2,1,0,3:T(2,128)(2,1)}), bf16[4,24,2,128,128]{4,2,1,0,3:T(2,128)(2,1)}, u32[]{:S(2)}, u32[]{:S(2)}) async-start(bf16[4,24,2,128,128]{4,2,1,0,3:T(2,128)(2,1)} %copy.24), calls=%async_computation | async-start | bytes 12582912 | tf_op jit(solution)/shard_map/all_to_all | solution.py:50
  52.5 136.8 %all-to-all-done = bf16[4,24,2,128,128]{4,2,1,0,3:T(2,128)(2,1)} async-done(((bf16[4,24,2,128,128]{4,2,1,0,3:T(2,128)(2,1)}), bf16[4,24,2,128,128]{4,2,1,0,3:T(2,128)(2,1)}, u32[]{:S(2)}, u32[]{:S(2)}) %all-to-all-start) | async-done | bytes 6291488 | tf_op jit(solution)/shard_map/all_to_all | solution.py:50
  189.4 10.1 %copy.25 = bf16[4,24,2,128,128]{4,3,2,1,0:T(8,128)(2,1)S(1)} copy(bf16[4,24,2,128,128]{4,2,1,0,3:T(2,128)(2,1)} %all-to-all-done) | data formatting | bytes 12582912 | tf_op jit(solution)/shard_map/all_to_all | solution.py:50
  199.4 4.4 copy.26
  203.8 8.5 %convert_bitcast_fusion = bf16[4,192,2,16,128]{4,1,2,0,3:T(8,128)(2,1)} fusion(bf16[192,16,128,1,1]{2,0,4,3,1:T(8,128)(2,1)S(1)} %bitcast.61, f32[128,128]{0,1:T(8,128)S(1)} %add_divide_fusion, f32[16,128]{1,0:T(8,128)S(1)} %fusion.27, bf16[4,192,2,16,128]{4,3,2,1,0:T(8,128)(2,1)} %bitcast.59), kind=kOutput, calls=%fused_computation.13 | convolution fusion | flops 1620049920 | bytes 13443072 | tf_op jit(solution)/shard_map/lmn,brmnc->blrmc/dot_general | solution.py:55
  212.3 9.5 %copy.31 = bf16[4,192,2,16,128]{4,2,0,3,1:T(2,128)(2,1)S(1)} copy(bf16[4,192,2,16,128]{4,1,2,0,3:T(8,128)(2,1)} %convert_bitcast_fusion) | data formatting | bytes 12582912 | tf_op jit(solution)/shard_map/convert_element_type | solution.py:57
  221.8 141.7 %all_to_all.51 = bf16[4,192,2,16,128]{4,2,0,3,1:T(2,128)(2,1)S(1)} all-to-all(bf16[4,192,2,16,128]{4,2,0,3,1:T(2,128)(2,1)S(1)} %copy.31), channel_id=1, replica_groups=mesh['grp'=4,'lat'=8] {'lat'}, dimensions={1} | all-to-all | bytes 12582912 | tf_op jit(solution)/shard_map/all_to_all | solution.py:58
  363.5 1.8 copy.32
  365.3 2.7 fusion.25
  368.0 6.4 %copy-done.2 = f32[384,4,24,128]{3,0,2,1:T(8,128)} copy-done((f32[384,4,24,128]{3,0,2,1:T(8,128)}, f32[384,4,24,128]{3,0,2,1:T(8,128)S(1)}, u32[]{:S(2)}) %copy-start.2) | copy-done | bytes 18874392
  374.5 4.3 bitcast_convert_fusion
  378.8 17.0 %fusion.36 = f32[36864,256]{1,0:T(8,128)} fusion(bf16[36864,128]{1,0:T(8,128)(2,1)} %bitcast_convert_fusion, bf16[128,256]{1,0:T(8,128)(2,1)S(1)} %copy-done.3), kind=kOutput, calls=%fused_computation.46 | convolution fusion | flops 2415919104 | bytes 47251456 | tf_op jit(solution)/shard_map/dot_general | solution.py:65
  395.7 27.9 %fusion.2 = f32[36864,256]{1,0:T(8,128)} fusion(bf16[256,256]{1,0:T(8,128)(2,1)S(1)} %copy-done, f32[36864,256]{1,0:T(8,128)} %fusion.36, bf16[36864,128]{1,0:T(8,128)(2,1)} %bitcast.62, bf16[128,256]{1,0:T(8,128)(2,1)S(1)} %copy-done.5, f32[256]{0:T(256)S(1)} %copy-done.7), kind=kOutput, calls=%fused_computation.8 | convolution fusion | flops 7313817600 | bytes 85132288 | tf_op jit(solution)/shard_map/dot_general | solution.py:73
  423.6 24.7 %fusion.1 = bf16[36864,128]{1,0:T(8,128)(2,1)} fusion(f32[36864,128]{1,0:T(8,128)} %bitcast.51, bf16[256,128]{1,0:T(8,128)(2,1)S(1)} %copy-done.6, f32[36864,256]{1,0:T(8,128)} %fusion.2), kind=kOutput, calls=%fused_computation.3 | convolution fusion | flops 2472542208 | bytes 66125824 | tf_op jit(solution)/shard_map/dot_general | solution.py:75
  448.3 7.6 %reduce_sum.21 = bf16[24,384,128]{2,1,0:T(8,128)(2,1)} reduce(bf16[4,24,384,128]{3,2,1,0:T(8,128)(2,1)} %bitcast.53, bf16[]{:T(256)} %constant.37.clone.1), dimensions={0}, to_apply=%region_0.1 | reduce | flops 3538944 | bytes 11796482 | tf_op jit(solution)/shard_map/reduce_sum | solution.py:79
  455.9 54.8 %all-reduce.3.cloned.1.call-done = bf16[24,384,128]{2,1,0:T(8,128)(2,1)} async-done(((bf16[24,384,128]{2,1,0:T(8,128)(2,1)}), bf16[24,384,128]{2,1,0:T(8,128)(2,1)}) %all-reduce.3.cloned.1.call-update) | async-done | bytes 2359312 | tf_op jit(solution)/shard_map/psum | solution.py:79
  510.7 4.4 convert_multiply_fusion.1
  515.2 9.8 %multiply_reduce_fusion = bf16[24,384,128]{2,1,0:T(8,128)(2,1)} fusion(bf16[4,24,384,128]{3,2,1,0:T(8,128)(2,1)} %bitcast.54, f32[24,384,128]{2,1,0:T(8,128)} %convert_multiply_fusion.1), kind=kLoop, calls=%fused_computation.7 | loop fusion | flops 17694720 | bytes 16515072 | tf_op jit(solution)/shard_map/reduce_sum | solution.py:84
  525.0 55.9 %all-reduce.5.cloned.1.call-done = bf16[24,384,128]{2,1,0:T(8,128)(2,1)} async-done(((bf16[24,384,128]{2,1,0:T(8,128)(2,1)}), bf16[24,384,128]{2,1,0:T(8,128)(2,1)}) %all-reduce.5.cloned.1.call-update) | async-done | bytes 2359312 | tf_op jit(solution)/shard_map/psum | solution.py:83
  580.8 4.4 convert_multiply_fusion
  (26 shorter events, 1.7 us)
Async XLA Ops:
  7.2 388.6 %copy-start = (bf16[256,256]{1,0:T(8,128)(2,1)S(1)}, bf16[256,256]{1,0:T(8,128)(2,1)}, u32[]{:S(2)}) copy-start(bf16[256,256]{1,0:T(8,128)(2,1)} %param.16) | copy-start | bytes 393220
  9.7 35.8 %all-to-all-start.1 = ((bf16[24,128,128]{2,0,1:T(8,128)(2,1)}), bf16[24,128,128]{2,0,1:T(8,128)(2,1)S(1)}, u32[]{:S(2)}, u32[]{:S(2)}) async-start(bf16[24,128,128]{2,0,1:T(8,128)(2,1)} %copy.27), calls=%async_computation.1 | async-start | bytes 1572864 | tf_op jit(solution)/shard_map/all_to_all | solution.py:42
  45.6 6.7 %copy-start.4 = (f32[128]{0:T(128)S(1)}, f32[128]{0:T(128)}, u32[]{:S(2)}) copy-start(f32[128]{0:T(128)} %param.12) | copy-start | bytes 1540
  45.6 143.8 %all-to-all-start = ((bf16[4,24,2,128,128]{4,2,1,0,3:T(2,128)(2,1)}), bf16[4,24,2,128,128]{4,2,1,0,3:T(2,128)(2,1)}, u32[]{:S(2)}, u32[]{:S(2)}) async-start(bf16[4,24,2,128,128]{4,2,1,0,3:T(2,128)(2,1)} %copy.24), calls=%async_computation | async-start | bytes 12582912 | tf_op jit(solution)/shard_map/all_to_all | solution.py:50
  51.7 459.0 %all-reduce.3.cloned.1.call-start = ((), (), s32[]{:S(2)}) async-start(), calls=%async_computation.3 | async-start | bytes 4718592 | tf_op jit(solution)/shard_map/psum | solution.py:79
  368.0 6.5 %copy-start.2 = (f32[384,4,24,128]{3,0,2,1:T(8,128)}, f32[384,4,24,128]{3,0,2,1:T(8,128)S(1)}, u32[]{:S(2)}) copy-start(f32[384,4,24,128]{3,0,2,1:T(8,128)S(1)} %fusion.25) | copy-start | bytes 56623108
  374.5 4.3 copy-start.3
  378.8 17.0 %copy-start.5 = (bf16[128,256]{1,0:T(8,128)(2,1)S(1)}, bf16[128,256]{1,0:T(8,128)(2,1)}, u32[]{:S(2)}) copy-start(bf16[128,256]{1,0:T(8,128)(2,1)} %param.14) | copy-start | bytes 196612
  378.8 17.0 %copy-start.7 = (f32[256]{0:T(256)S(1)}, f32[256]{0:T(256)}, u32[]{:S(2)}) copy-start(f32[256]{0:T(256)} %param.15) | copy-start | bytes 3076
  395.7 27.9 %copy-start.6 = (bf16[256,128]{1,0:T(8,128)(2,1)S(1)}, bf16[256,128]{1,0:T(8,128)(2,1)}, u32[]{:S(2)}) copy-start(bf16[256,128]{1,0:T(8,128)(2,1)} %param.17) | copy-start | bytes 196612
  455.9 125.0 %all-reduce.5.cloned.1.call-start = ((), (), s32[]{:S(2)}) async-start(), calls=%async_computation.4 | async-start | bytes 4718592 | tf_op jit(solution)/shard_map/psum | solution.py:83
  510.7 74.6 %copy-start.1 = (bf16[256,256]{1,0:T(8,128)(2,1)S(1)}, bf16[256,256]{1,0:T(8,128)(2,1)}, u32[]{:S(2)}) copy-start(bf16[256,256]{1,0:T(8,128)(2,1)} %param.16) | copy-start | bytes 393220
Sparse Core Ops, SparseCore 0:
  456.0 54.6 all-reduce.2
  525.1 55.7 all-reduce.4
where the time goes:
time: 597 us; the launch traced here: 592 us
  waiting for transfers between devices  248 us (42%)
  blocking collectives  142 us (24%)
  matrix products  88 us (15%)
  local copies, waits for them, and re-layouts  55.2 us (9%)
  other arithmetic  31.5 us (5%)
  between operations  14.4 us (2%)
  starting transfers between devices  14 us (2%)
    all_to_all x1, blocking collectives, per_device(): lax.all_to_all(banded_grid, 'lat', split_axis=1, concat_axis=3, tiled=True)  142 us
    all_to_all x1, waiting for transfers between devices, per_device(): lax.all_to_all(fourier, 'lat', split_axis=3, concat_axis=1, tiled=True)  137 us
    psum x1, waiting for transfers between devices, per_device(): lax.psum(jnp.sum(jnp.square(member_values - ens_mean), axis=0).astype(jnp...  55.9 us
    psum x1, waiting for transfers between devices, per_device(): lax.psum(jnp.sum(member_values, axis=0).astype(jnp.bfloat16), 'grp')  54.8 us
    dot_general x1, matrix products, per_device(): jnp.dot(hidden_one, middle_weight, preferred_element_type=jnp.float32)  27.9 us
    dot_general x1, matrix products, per_device(): jnp.dot(hidden_two, output_weight, preferred_element_type=jnp.float32)  24.7 us
    reshape x1, local copies, waits for them, and re-layouts, per_device(): fourier = fourier.reshape(members, lat_rows, 2, wave_count, channels)  20.3 us
    dot_general x1, matrix products, per_device(): jnp.dot(smoothed_in, input_weight, preferred_element_type=jnp.float32)  17 us
  transfers between devices with their start and end apart: 4, of which 3 were waited for; matrix products, arithmetic and copies ran while one was open for 5% of the time, Pallas kernels for 0%

commit v1 on v0

--- a/solution.py
+++ b/solution.py
@@ -47,7 +47,12 @@
     spectrum = jnp.einsum(
         "lmn,blrmc->brmnc",
         basis_band,
-        lax.all_to_all(fourier, "lat", split_axis=3, concat_axis=1, tiled=True),
+        jnp.concatenate(
+            lax.all_to_all(
+                jnp.stack(jnp.split(fourier, lax.axis_size("lat"), axis=3)), "lat", 0, 0
+            ),
+            axis=1,
+        ),
         preferred_element_type=jnp.float32,
     )
     spectrum = spectrum * triangle[None, None, :, :, None]

time: 597 us -> 575 us (0.963)
  local copies, waits for them, and re-layouts: 55.2 us -> 36.4 us
    reshape x1 -> x0, local copies, waits for them, and re-layouts: 20.3 us -> none  [per_device(): fourier = fourier.reshape(members, lat_rows, 2, wave_count, channels)]
    unnamed x17 -> x24, local copies, waits for them, and re-layouts: 9.04 us -> 16.6 us
    all_to_all x2 -> x1, local copies, waits for them, and re-layouts: 14.4 us -> 7.25 us  [per_device(): lax.all_to_all(jnp.stack(jnp.split(fourier, lax.axis_size('lat'), axis=3)...]
  transfers between devices with their start and end apart: 4 -> 4, of which waited for: 3 -> 4; matrix products, arithmetic and copies ran while one was open for 5% -> 3% of each run, Pallas kernels for 0% -> 0%
where the time goes in v1:
time: 575 us; the launch traced here: 574 us
  waiting for transfers between devices  251 us (44%)
  blocking collectives  142 us (25%)
  matrix products  87.9 us (15%)
  local copies, waits for them, and re-layouts  36.4 us (6%)
  other arithmetic  31.5 us (5%)
  between operations  14.1 us (2%)
  starting transfers between devices  12.1 us (2%)
    all_to_all x1, blocking collectives, per_device(): lax.all_to_all(banded_grid, 'lat', split_axis=1, concat_axis=3, tiled=True)  142 us
    all_to_all x1, waiting for transfers between devices, per_device(): lax.all_to_all(jnp.stack(jnp.split(fourier, lax.axis_size('lat'), axis=3)...  137 us
    psum x1, waiting for transfers between devices, per_device(): lax.psum(jnp.sum(jnp.square(member_values - ens_mean), axis=0).astype(jnp...  55.9 us
    psum x1, waiting for transfers between devices, per_device(): lax.psum(jnp.sum(member_values, axis=0).astype(jnp.bfloat16), 'grp')  54.8 us
    dot_general x1, matrix products, per_device(): jnp.dot(hidden_one, middle_weight, preferred_element_type=jnp.float32)  27.9 us
    dot_general x1, matrix products, per_device(): jnp.dot(hidden_two, output_weight, preferred_element_type=jnp.float32)  24.7 us
    dot_general x1, matrix products, per_device(): jnp.dot(smoothed_in, input_weight, preferred_element_type=jnp.float32)  17 us
    unnamed x24, local copies, waits for them, and re-layouts  16.6 us
  transfers between devices with their start and end apart: 4, of which 4 were waited for; matrix products, arithmetic and copies ran while one was open for 3% of the time, Pallas kernels for 0%

profile of v1, /device:TPU:0, one launch (start us, length us, event | category | flops | bytes accessed | tf_op | source)
XLA Modules:
  0.0 574.5 jit_solution(5132565784148475371)
XLA Ops:
  7.2 2.6 copy.26
  9.7 7.3 %all-to-all-start.1 = ((bf16[24,128,128]{2,0,1:T(8,128)(2,1)}), bf16[24,128,128]{2,0,1:T(8,128)(2,1)S(1)}, u32[]{:S(2)}, u32[]{:S(2)}) async-start(bf16[24,128,128]{2,0,1:T(8,128)(2,1)} %copy.26), calls=%async_computation.1 | async-start | bytes 1572864 | tf_op jit(solution)/shard_map/all_to_all | solution.py:42
  17.9 7.4 %convolution_convert_fusion = bf16[256,4,24,128]{3,0,2,1:T(8,128)(2,1)S(1)} fusion(bf16[4,24,384,128]{3,2,1,0:T(8,128)(2,1)} %param.9, f32[384,128]{0,1:T(8,128)S(1)} %get-tuple-element.3, f32[384,128]{0,1:T(8,128)S(1)} %get-tuple-element.4), kind=kOutput, calls=%fused_computation.19 | convolution fusion | flops 2419359744 | bytes 16121856 | tf_op jit(solution)/shard_map/blxc,xk->blkc/dot_general | solution.py:38
  26.3 1.1 fusion.22
  33.9 3.3 all-to-all-done.1
  37.2 4.7 all-to-all-start
  42.3 136.9 %all-to-all-done = bf16[8,4,24,2,16,128]{5,4,3,2,1,0:T(8,128)(2,1)} async-done(((bf16[8,4,24,2,16,128]{5,4,3,2,1,0:T(8,128)(2,1)}), bf16[8,4,24,2,16,128]{5,4,3,2,1,0:T(8,128)(2,1)}, u32[]{:S(2)}, u32[]{:S(2)}) %all-to-all-start) | async-done | bytes 6291488 | tf_op jit(solution)/shard_map/all_to_all | solution.py:51
  179.2 7.2 %copy.25 = bf16[8,4,24,2,16,128]{5,4,3,2,0,1:T(8,128)(2,1)} copy(bf16[8,4,24,2,16,128]{5,4,3,2,1,0:T(8,128)(2,1)} %all-to-all-done) | data formatting | bytes 12582912 | tf_op jit(solution)/shard_map/all_to_all | solution.py:51
  186.4 8.4 %convert_bitcast_fusion = bf16[4,192,2,16,128]{4,1,2,0,3:T(8,128)(2,1)} fusion(bf16[192,16,128,1,1]{2,0,4,3,1:T(8,128)(2,1)S(1)} %bitcast.98, f32[128,128]{0,1:T(8,128)S(1)} %add_divide_fusion, f32[16,128]{1,0:T(8,128)S(1)} %fusion.35, bf16[4,192,2,16,128]{4,3,2,1,0:T(8,128)(2,1)} %bitcast.96), kind=kOutput, calls=%fused_computation.13 | convolution fusion | flops 1620049920 | bytes 13443072 | tf_op jit(solution)/shard_map/lmn,brmnc->blrmc/dot_general | solution.py:60
  194.8 9.5 %copy.30 = bf16[4,192,2,16,128]{4,2,0,3,1:T(2,128)(2,1)S(1)} copy(bf16[4,192,2,16,128]{4,1,2,0,3:T(8,128)(2,1)} %convert_bitcast_fusion) | data formatting | bytes 12582912 | tf_op jit(solution)/shard_map/convert_element_type | solution.py:62
  204.3 141.6 %all_to_all.38 = bf16[4,192,2,16,128]{4,2,0,3,1:T(2,128)(2,1)S(1)} all-to-all(bf16[4,192,2,16,128]{4,2,0,3,1:T(2,128)(2,1)S(1)} %copy.30), channel_id=1, replica_groups=mesh['grp'=4,'lat'=8] {'lat'}, dimensions={1} | all-to-all | bytes 12582912 | tf_op jit(solution)/shard_map/all_to_all | solution.py:63
  345.9 1.8 copy.31
  347.8 2.7 fusion.33
  350.4 6.4 %copy-done.2 = f32[384,4,24,128]{3,0,2,1:T(8,128)} copy-done((f32[384,4,24,128]{3,0,2,1:T(8,128)}, f32[384,4,24,128]{3,0,2,1:T(8,128)S(1)}, u32[]{:S(2)}) %copy-start.2) | copy-done | bytes 18874392
  356.9 4.3 bitcast_convert_fusion
  361.2 17.0 %fusion.44 = f32[36864,256]{1,0:T(8,128)} fusion(bf16[36864,128]{1,0:T(8,128)(2,1)} %bitcast_convert_fusion, bf16[128,256]{1,0:T(8,128)(2,1)S(1)} %copy-done.3), kind=kOutput, calls=%fused_computation.62 | convolution fusion | flops 2415919104 | bytes 47251456 | tf_op jit(solution)/shard_map/dot_general | solution.py:70
  378.1 27.9 %fusion.2 = f32[36864,256]{1,0:T(8,128)} fusion(bf16[256,256]{1,0:T(8,128)(2,1)S(1)} %copy-done, f32[36864,256]{1,0:T(8,128)} %fusion.44, bf16[36864,128]{1,0:T(8,128)(2,1)} %bitcast.99, bf16[128,256]{1,0:T(8,128)(2,1)S(1)} %copy-done.5, f32[256]{0:T(256)S(1)} %copy-done.7), kind=kOutput, calls=%fused_computation.8 | convolution fusion | flops 7313817600 | bytes 85132288 | tf_op jit(solution)/shard_map/dot_general | solution.py:78
  406.0 24.7 %fusion.1 = bf16[36864,128]{1,0:T(8,128)(2,1)} fusion(f32[36864,128]{1,0:T(8,128)} %bitcast.82, bf16[256,128]{1,0:T(8,128)(2,1)S(1)} %copy-done.6, f32[36864,256]{1,0:T(8,128)} %fusion.2), kind=kOutput, calls=%fused_computation.3 | convolution fusion | flops 2472542208 | bytes 66125824 | tf_op jit(solution)/shard_map/dot_general | solution.py:80
  430.7 7.6 %reduce_sum.21 = bf16[24,384,128]{2,1,0:T(8,128)(2,1)} reduce(bf16[4,24,384,128]{3,2,1,0:T(8,128)(2,1)} %bitcast.91, bf16[]{:T(256)} %constant.37.clone.1), dimensions={0}, to_apply=%region_0.1 | reduce | flops 3538944 | bytes 11796482 | tf_op jit(solution)/shard_map/reduce_sum | solution.py:84
  438.3 54.8 %all-reduce.3.cloned.1.call-done = bf16[24,384,128]{2,1,0:T(8,128)(2,1)} async-done(((bf16[24,384,128]{2,1,0:T(8,128)(2,1)}), bf16[24,384,128]{2,1,0:T(8,128)(2,1)}) %all-reduce.3.cloned.1.call-update) | async-done | bytes 2359312 | tf_op jit(solution)/shard_map/psum | solution.py:84
  493.1 4.4 convert_multiply_fusion.1
  497.5 9.8 %multiply_reduce_fusion = bf16[24,384,128]{2,1,0:T(8,128)(2,1)} fusion(bf16[4,24,384,128]{3,2,1,0:T(8,128)(2,1)} %bitcast.92, f32[24,384,128]{2,1,0:T(8,128)} %convert_multiply_fusion.1), kind=kLoop, calls=%fused_computation.7 | loop fusion | flops 17694720 | bytes 16515072 | tf_op jit(solution)/shard_map/reduce_sum | solution.py:89
  507.3 55.9 %all-reduce.5.cloned.1.call-done = bf16[24,384,128]{2,1,0:T(8,128)(2,1)} async-done(((bf16[24,384,128]{2,1,0:T(8,128)(2,1)}), bf16[24,384,128]{2,1,0:T(8,128)(2,1)}) %all-reduce.5.cloned.1.call-update) | async-done | bytes 2359312 | tf_op jit(solution)/shard_map/psum | solution.py:88
  563.2 4.4 convert_multiply_fusion
  (32 shorter events, 8.8 us)
Async XLA Ops:
  7.2 371.0 %copy-start = (bf16[256,256]{1,0:T(8,128)(2,1)S(1)}, bf16[256,256]{1,0:T(8,128)(2,1)}, u32[]{:S(2)}) copy-start(bf16[256,256]{1,0:T(8,128)(2,1)} %param.16) | copy-start | bytes 393220
  9.7 27.5 %all-to-all-start.1 = ((bf16[24,128,128]{2,0,1:T(8,128)(2,1)}), bf16[24,128,128]{2,0,1:T(8,128)(2,1)S(1)}, u32[]{:S(2)}, u32[]{:S(2)}) async-start(bf16[24,128,128]{2,0,1:T(8,128)(2,1)} %copy.26), calls=%async_computation.1 | async-start | bytes 1572864 | tf_op jit(solution)/shard_map/all_to_all | solution.py:42
  33.9 8.2 %copy-start.4 = (f32[128]{0:T(128)S(1)}, f32[128]{0:T(128)}, u32[]{:S(2)}) copy-start(f32[128]{0:T(128)} %param.12) | copy-start | bytes 1540
  37.2 142.0 %all-to-all-start = ((bf16[8,4,24,2,16,128]{5,4,3,2,1,0:T(8,128)(2,1)}), bf16[8,4,24,2,16,128]{5,4,3,2,1,0:T(8,128)(2,1)}, u32[]{:S(2)}, u32[]{:S(2)}) async-start(bf16[8,4,24,2,16,128]{5,4,3,2,1,0:T(8,128)(2,1)} %fusion.16), calls=%async_computation | async-start | bytes 12582912 | tf_op jit(solution)/shard_map/all_to_all | solution.py:51
  42.0 451.2 %all-reduce.3.cloned.1.call-start = ((), (), s32[]{:S(2)}) async-start(), calls=%async_computation.3 | async-start | bytes 4718592 | tf_op jit(solution)/shard_map/psum | solution.py:84
  350.4 6.5 %copy-start.2 = (f32[384,4,24,128]{3,0,2,1:T(8,128)}, f32[384,4,24,128]{3,0,2,1:T(8,128)S(1)}, u32[]{:S(2)}) copy-start(f32[384,4,24,128]{3,0,2,1:T(8,128)S(1)} %fusion.33) | copy-start | bytes 56623108
  356.9 4.3 copy-start.3
  361.2 17.0 %copy-start.5 = (bf16[128,256]{1,0:T(8,128)(2,1)S(1)}, bf16[128,256]{1,0:T(8,128)(2,1)}, u32[]{:S(2)}) copy-start(bf16[128,256]{1,0:T(8,128)(2,1)} %param.14) | copy-start | bytes 196612
  361.2 17.0 %copy-start.7 = (f32[256]{0:T(256)S(1)}, f32[256]{0:T(256)}, u32[]{:S(2)}) copy-start(f32[256]{0:T(256)} %param.15) | copy-start | bytes 3076
  378.1 27.9 %copy-start.6 = (bf16[256,128]{1,0:T(8,128)(2,1)S(1)}, bf16[256,128]{1,0:T(8,128)(2,1)}, u32[]{:S(2)}) copy-start(bf16[256,128]{1,0:T(8,128)(2,1)} %param.17) | copy-start | bytes 196612
  438.3 124.9 %all-reduce.5.cloned.1.call-start = ((), (), s32[]{:S(2)}) async-start(), calls=%async_computation.4 | async-start | bytes 4718592 | tf_op jit(solution)/shard_map/psum | solution.py:88
  497.5 70.1 %copy-start.1 = (bf16[256,256]{1,0:T(8,128)(2,1)S(1)}, bf16[256,256]{1,0:T(8,128)(2,1)}, u32[]{:S(2)}) copy-start(bf16[256,256]{1,0:T(8,128)(2,1)} %param.16) | copy-start | bytes 393220
Sparse Core Ops, SparseCore 0:
  438.4 54.6 all-reduce.2
  507.4 55.7 all-reduce.4
